TPU v7x, 32 devices: a whole 2x2x4 slice. The times are simulated.
32 devices in a mesh: blk: 4 (over y, x), rows: 8 (over z, core).
Axes of the slice: x: 2, y: 2, z: 4, core: 2. Of those that a mesh axis runs over, the one named last changes fastest.
Arguments:
- embeddings: bfloat16 [65536, 768], P(('blk', 'rows')), may hold values from -6 to 6
- coverage: float32 [65536], P(('blk', 'rows')), may hold values from 0 to 4
- chosen_index: int32 [64], replicated, may hold values from 0 to 65535, as said below
- candidate_index: int32 [512], P('blk'), may hold values from 0 to 65535, as said below
Outputs:
- new_coverage: float32 [65536], P(('blk', 'rows'))
- gains: float32 [512], P(('blk', 'rows'))
Inputs may be any that keep to these rules, and one draw needn't show every extreme that they name: `chosen_index`: the entries are distinct; the rows r * 2048 to (r + 1) * 2048 - 1 hold at most 4 of them for every r, and exactly 4 for some r. `candidate_index`: entries b * 128 to (b + 1) * 128 - 1 lie in rows b * 16384 to (b + 1) * 16384 - 1.
All inputs are finite; a program needn't handle non-finite values.
Results may differ from a plain program's by a relative error of at most 0.00035.
Values may be sent and summed in bfloat16 or wider, within the bound.
A program may use at most 64 MiB of HBM per device.

v0:
```python
import jax
import jax.numpy as jnp
from jax import lax
from jax.sharding import PartitionSpec as P


def owned_rows(embeddings, indices, base_row):
    local_rows = embeddings.shape[0]
    offset = indices - base_row
    inside = (offset >= 0) & (offset < local_rows)
    safe = jnp.clip(offset, 0, local_rows - 1)
    picked = jnp.take(embeddings, safe, axis=0).astype(jnp.float32)
    return jnp.where(inside[:, None], picked, 0.0)


def local(embeddings, coverage, chosen_index, candidate_index):
    local_rows = embeddings.shape[0]
    width = embeddings.shape[1]
    scale = 1.0 / width**0.5
    device_pos = lax.axis_index("blk") * lax.axis_size("rows") + lax.axis_index("rows")
    base_row = device_pos * local_rows
    chosen_f = lax.psum(owned_rows(embeddings, chosen_index, base_row), ("blk", "rows"))
    chosen_rows = chosen_f.astype(jnp.bfloat16)
    sims = jnp.dot(embeddings, chosen_rows.T, preferred_element_type=jnp.float32) * scale
    best = jnp.max(sims, axis=1)
    new_coverage = jnp.maximum(coverage, best)
    block_f = lax.psum(
        owned_rows(embeddings, candidate_index, base_row).astype(jnp.bfloat16), "rows"
    )
    cand_sims = (
        jnp.dot(
            embeddings,
            lax.all_gather(block_f, "blk", axis=0, tiled=True).T,
            preferred_element_type=jnp.float32,
        )
        * scale
    )
    gain_part = jnp.sum(jnp.maximum(cand_sims - new_coverage[:, None], 0.0), axis=0)
    gains = lax.psum_scatter(gain_part, ("blk", "rows"), scatter_dimension=0, tiled=True)
    return (new_coverage, gains)


def solution(mesh):
    placed = (P(("blk", "rows"), None), P(("blk", "rows")), P(), P("blk"))
    return jax.shard_map(
        local,
        mesh=mesh,
        in_specs=placed,
        out_specs=(P(("blk", "rows")), P(("blk", "rows"))),
        check_vma=False,
    )
```

profile of v0, /device:TPU:0, one launch (start us, length us, event | category | flops | bytes accessed | tf_op | source)
XLA Modules:
  0.0 129.1 jit_solution(3781930005201907829)
XLA Ops:
  7.2 0.0 copy-start
  7.2 0.0 all-reduce.4.cloned.1.call-start
  7.2 0.8 compare_and_fusion
  8.1 1.0 copy-done
  9.1 0.0 copy-start.1
  9.1 0.9 gather_fusion.1
  9.9 0.8 select_convert_fusion
  10.8 0.0 all-reduce.4.cloned.1.call-update
  10.8 0.7 compare_and_fusion.2
  11.5 0.7 gather_fusion
  12.2 0.1 convert_select_fusion
  12.3 44.4 %all-reduce.5 = bf16[64,768]{1,0:T(8,128)(2,1)S(1)} all-reduce(f32[64,768]{1,0:T(8,128)S(1)} %convert_select_fusion), channel_id=1, replica_groups=mesh['blk'=4,'rows'=8] {'blk','rows'}, use_global_device_ids=true, to_apply=%region_0.1 | all-reduce | flops 49152 | bytes 294912 | tf_op jit(solution)/shard_map/psum | solution.py:22
  56.7 1.1 fusion
  57.8 0.0 copy-done.1
  57.8 0.0 copy-start.2
  57.8 11.1 %all-reduce.4.cloned.1.call-done = bf16[128,768]{1,0:T(8,128)(2,1)} async-done(((bf16[128,768]{1,0:T(8,128)(2,1)}), bf16[128,768]{1,0:T(8,128)(2,1)}) %all-reduce.4.cloned.1.call-update) | async-done | bytes 196624 | tf_op jit(solution)/shard_map/psum | solution.py:27
  68.9 12.4 %all_gather.3 = bf16[512,768]{1,0:T(8,128)(2,1)S(1)} all-gather(bf16[128,768]{1,0:T(8,128)(2,1)} %all-reduce.4.cloned.1.call-done), channel_id=1, replica_groups=mesh['blk'=4,'rows'=8] {'blk'}, dimensions={0}, use_global_device_ids=true | all-gather | bytes 983040 | tf_op jit(solution)/shard_map/all_gather | solution.py:33
  81.3 1.9 %maximum_reduce_fusion = f32[512]{0:T(512)S(1)} fusion(bf16[512,768]{1,0:T(8,128)(2,1)S(1)} %all_gather.3, bf16[2048,768]{1,0:T(8,128)(2,1)S(1)} %copy-done, f32[2048]{0:T(1024)S(1)} %max.18), kind=kOutput, calls=%fused_computation.2 | convolution fusion | flops 1614806528 | bytes 3942400 | tf_op jit(solution)/shard_map/dot_general | solution.py:31
  83.3 0.0 copy-done.2
  83.3 38.4 %all-reduce = f32[512]{0:T(512)S(1)} all-reduce(f32[512]{0:T(512)S(1)} %maximum_reduce_fusion), channel_id=2, replica_groups=mesh['blk'=4,'rows'=8] {'blk','rows'}, use_global_device_ids=true, to_apply=%region_4.5.clone | all-reduce | flops 512 | bytes 4096
  121.6 0.6 dynamic-slice
  (3 shorter events, 0.0 us)
Async XLA Ops:
  7.2 1.9 %copy-start = (bf16[2048,768]{1,0:T(8,128)(2,1)S(1)}, bf16[2048,768]{1,0:T(8,128)(2,1)}, u32[]{:S(2)}) copy-start(bf16[2048,768]{1,0:T(8,128)(2,1)} %param.4) | copy-start | bytes 9437188
  7.2 61.7 %all-reduce.4.cloned.1.call-start = ((), (), s32[]{:S(2)}) async-start(), calls=%async_computation | async-start | bytes 393216 | tf_op jit(solution)/shard_map/psum | solution.py:27
  9.1 48.7 %copy-start.1 = (f32[2048]{0:T(1024)S(1)}, f32[2048]{0:T(1024)}, u32[]{:S(2)}) copy-start(f32[2048]{0:T(1024)} %param.5) | copy-start | bytes 24580
  57.8 25.5 %copy-start.2 = (f32[2048]{0:T(1024)}, f32[2048]{0:T(1024)S(1)}, u32[]{:S(2)}) copy-start(f32[2048]{0:T(1024)S(1)} %max.18) | copy-start | bytes 24580
Sparse Core Ops, SparseCore 0:
  10.9 57.9 all-reduce.3
where the time goes:
time: 129 us
  blocking collectives  95.2 us (74%)
  between operations  14.1 us (11%)
  waiting for transfers between devices  11.1 us (9%)
  local copies, waits for them, and re-layouts  3.2 us (2%)
  matrix products  3 us (2%)
  other arithmetic  2.41 us (2%)
    psum x1, blocking collectives, local(): lax.psum(owned_rows(embeddings, chosen_index, base_row), ('blk', 'rows'))  44.4 us
    unnamed x1, blocking collectives  38.4 us
    all_gather x1, blocking collectives, local(): lax.all_gather(block_f, 'blk', axis=0, tiled=True)  12.4 us
    psum x1, waiting for transfers between devices, local(): lax.psum(owned_rows(embeddings, candidate_index, base_row).astype(jnp.bfl...  11.1 us
  transfers between devices with their start and end apart: 1, of which 1 were waited for; matrix products, arithmetic and copies ran while one was open for 2% of the time, Pallas kernels for 0%

commit v1 on v0

--- a/solution.py
+++ b/solution.py
@@ -19,7 +19,7 @@
     scale = 1.0 / width**0.5
     device_pos = lax.axis_index("blk") * lax.axis_size("rows") + lax.axis_index("rows")
     base_row = device_pos * local_rows
-    chosen_f = lax.psum(owned_rows(embeddings, chosen_index, base_row), ("blk", "rows"))
+    chosen_f = lax.psum(lax.psum(owned_rows(embeddings, chosen_index, base_row), "rows"), "blk")
     chosen_rows = chosen_f.astype(jnp.bfloat16)
     sims = jnp.dot(embeddings, chosen_rows.T, preferred_element_type=jnp.float32) * scale
     best = jnp.max(sims, axis=1)

time: 129 us -> 186 us (1.44)
  waiting for transfers between devices: 11.1 us -> 91.5 us
  blocking collectives: 95.2 us -> 70.5 us
    psum x0 -> x1, waiting for transfers between devices: none -> 55.7 us  [local(): lax.psum(owned_rows(embeddings, chosen_index, base_row), 'rows')]
    psum x1, waiting for transfers between devices: 11.1 us -> 35.9 us  [local(): lax.psum(owned_rows(embeddings, candidate_index, base_row).astype(jnp.bfl...]
    psum x1, blocking collectives: 44.4 us -> 19.6 us  [local(): lax.psum(lax.psum(owned_rows(embeddings, chosen_index, base_row), 'rows')...]
  transfers between devices with their start and end apart: 1 -> 2, of which waited for: 1 -> 2; matrix products, arithmetic and copies ran while one was open for 2% -> 2% of each run, Pallas kernels for 0% -> 0%
where the time goes in v1:
time: 186 us; the launch traced here: 185 us
  waiting for transfers between devices  91.5 us (49%)
  blocking collectives  70.5 us (38%)
  between operations  14.1 us (8%)
  local copies, waits for them, and re-layouts  3.2 us (2%)
  other arithmetic  3.08 us (2%)
  matrix products  3 us (2%)
    psum x1, waiting for transfers between devices, local(): lax.psum(owned_rows(embeddings, chosen_index, base_row), 'rows')  55.7 us
    unnamed x1, blocking collectives  38.4 us
    psum x1, waiting for transfers between devices, local(): lax.psum(owned_rows(embeddings, candidate_index, base_row).astype(jnp.bfl...  35.9 us
    psum x1, blocking collectives, local(): lax.psum(lax.psum(owned_rows(embeddings, chosen_index, base_row), 'rows')...  19.6 us
    all_gather x1, blocking collectives, local(): lax.all_gather(block_f, 'blk', axis=0, tiled=True)  12.4 us
  transfers between devices with their start and end apart: 2, of which 2 were waited for; matrix products, arithmetic and copies ran while one was open for 2% of the time, Pallas kernels for 0%

profile of v1, /device:TPU:0, one launch (start us, length us, event | category | flops | bytes accessed | tf_op | source)
XLA Modules:
  0.0 185.5 jit_solution(1596013340467307572)
XLA Ops:
  7.2 0.0 copy-start
  7.2 0.0 all-reduce.5.cloned.1.call-start
  7.2 0.8 compare_and_fusion.2
  8.1 1.0 copy-done
  9.1 0.7 gather_fusion
  9.8 0.8 convert_select_fusion
  10.5 0.0 copy-start.1
  10.5 0.0 all-reduce.5.cloned.1.call-update
  10.6 0.0 all-reduce.7.cloned.1.call-start
  10.6 0.7 compare_and_fusion
  11.3 0.9 gather_fusion.1
  12.2 0.8 select_convert_fusion
  13.0 0.0 all-reduce.7.cloned.1.call-update
  13.0 55.7 %all-reduce.5.cloned.1.call-done = f32[64,768]{1,0:T(8,128)} async-done(((f32[64,768]{1,0:T(8,128)}), f32[64,768]{1,0:T(8,128)}) %all-reduce.5.cloned.1.call-update) | async-done | bytes 196624 | tf_op jit(solution)/shard_map/psum | solution.py:22
  68.7 19.6 %all-reduce.8 = bf16[64,768]{1,0:T(8,128)(2,1)S(1)} all-reduce(f32[64,768]{1,0:T(8,128)} %all-reduce.5.cloned.1.call-done), channel_id=1, replica_groups=mesh['blk'=4,'rows'=8] {'blk'}, use_global_device_ids=true, to_apply=%region_1.2 | all-reduce | flops 49152 | bytes 294912 | tf_op jit(solution)/shard_map/psum | solution.py:22
  88.3 1.1 fusion
  89.4 0.0 copy-done.1
  89.4 0.0 copy-start.2
  89.4 35.9 %all-reduce.7.cloned.1.call-done = bf16[128,768]{1,0:T(8,128)(2,1)} async-done(((bf16[128,768]{1,0:T(8,128)(2,1)}), bf16[128,768]{1,0:T(8,128)(2,1)}) %all-reduce.7.cloned.1.call-update) | async-done | bytes 196624 | tf_op jit(solution)/shard_map/psum | solution.py:27
  125.3 12.4 %all_gather.3 = bf16[512,768]{1,0:T(8,128)(2,1)S(1)} all-gather(bf16[128,768]{1,0:T(8,128)(2,1)} %all-reduce.7.cloned.1.call-done), channel_id=1, replica_groups=mesh['blk'=4,'rows'=8] {'blk'}, dimensions={0}, use_global_device_ids=true | all-gather | bytes 983040 | tf_op jit(solution)/shard_map/all_gather | solution.py:33
  137.7 1.9 %maximum_reduce_fusion = f32[512]{0:T(512)S(1)} fusion(bf16[512,768]{1,0:T(8,128)(2,1)S(1)} %all_gather.3, bf16[2048,768]{1,0:T(8,128)(2,1)S(1)} %copy-done, f32[2048]{0:T(1024)S(1)} %max.18), kind=kOutput, calls=%fused_computation.2 | convolution fusion | flops 1614806528 | bytes 3942400 | tf_op jit(solution)/shard_map/dot_general | solution.py:31
  139.7 0.0 copy-done.2
  139.7 38.4 %all-reduce = f32[512]{0:T(512)S(1)} all-reduce(f32[512]{0:T(512)S(1)} %maximum_reduce_fusion), channel_id=2, replica_groups=mesh['blk'=4,'rows'=8] {'blk','rows'}, use_global_device_ids=true, to_apply=%region_5.6.clone | all-reduce | flops 512 | bytes 4096
  178.0 0.6 dynamic-slice
  (3 shorter events, 0.0 us)
Async XLA Ops:
  7.2 1.9 %copy-start = (bf16[2048,768]{1,0:T(8,128)(2,1)S(1)}, bf16[2048,768]{1,0:T(8,128)(2,1)}, u32[]{:S(2)}) copy-start(bf16[2048,768]{1,0:T(8,128)(2,1)} %param.4) | copy-start | bytes 9437188
  7.2 61.5 %all-reduce.5.cloned.1.call-start = ((), (), s32[]{:S(2)}) async-start(), calls=%async_computation | async-start | bytes 393216 | tf_op jit(solution)/shard_map/psum | solution.py:22
  10.5 78.9 %copy-start.1 = (f32[2048]{0:T(1024)S(1)}, f32[2048]{0:T(1024)}, u32[]{:S(2)}) copy-start(f32[2048]{0:T(1024)} %param.5) | copy-start | bytes 24580
  10.6 114.7 %all-reduce.7.cloned.1.call-start = ((), (), s32[]{:S(2)}) async-start(), calls=%async_computation.1 | async-start | bytes 393216 | tf_op jit(solution)/shard_map/psum | solution.py:27
  89.4 50.2 %copy-start.2 = (f32[2048]{0:T(1024)}, f32[2048]{0:T(1024)S(1)}, u32[]{:S(2)}) copy-start(f32[2048]{0:T(1024)S(1)} %max.18) | copy-start | bytes 24580
Sparse Core Ops, SparseCore 0:
  10.7 57.9 all-reduce.4
  71.0 54.2 all-reduce.6
